TPU v7x, 8 devices: a whole 2x2x1 slice. The times are simulated.
8 devices in a mesh: dp: 2 (over y, z), sp: 4 (over x, core).
Axes of the slice: x: 2, y: 2, z: 1, core: 2. Of those that a mesh axis runs over, the one named last changes fastest.
Arguments:
- q: bfloat16 [64, 48, 128], P('dp'), parts along dimension 0
- k: bfloat16 [64, 8192, 8, 128], P('dp', 'sp'), parts along dimension 0
- v: bfloat16 [64, 8192, 8, 128], P('dp', 'sp'), parts along dimension 0
Outputs:
- q: bfloat16 [64, 48, 128], P('dp'), parts along dimension 0
There are 2 independent parts. A program takes and returns all parts, laid end to end along the dimension named above; each array names one.
All inputs are finite; a program needn't handle non-finite values.
Results may differ from a plain program's by a relative error of at most 0.012.
Values are sent between devices in bfloat16 or wider.
A program may use at most 2 GiB of HBM per device.

v0:
```python
import jax
import jax.numpy as jnp
from jax import lax
from jax.sharding import PartitionSpec as P


def einsum(form, a, b):
    return jnp.einsum(form, a.astype(jnp.float32), b.astype(jnp.float32))


def part_of(q, k, v):
    grouped = q.reshape(q.shape[0], k.shape[2], -1, q.shape[2])
    scores = einsum("bgsd,bugd->bgsu", grouped, k) * q.shape[2] ** -0.5
    high = jnp.max(scores, -1, keepdims=True)
    weights = jnp.exp(scores - high)
    seen = einsum("bgsu,bugd->bgsd", weights.astype(jnp.bfloat16), v)
    return jnp.concatenate([seen, jnp.sum(weights, -1, keepdims=True), high], -1)


def together(parts):
    seen, total, high = parts[..., :-2], parts[..., -2:-1], parts[..., -1:]
    scale = jnp.exp(high - jnp.max(high, 0))
    return (jnp.sum(seen * scale, 0) / jnp.sum(total * scale, 0)).astype(jnp.bfloat16)


def solution(mesh):
    def step(q, k, v):
        return together(lax.all_gather(part_of(q, k, v), "sp")).reshape(q.shape)

    return jax.shard_map(
        step,
        mesh=mesh,
        in_specs=(P("dp", None, None), P("dp", "sp", None, None), P("dp", "sp", None, None)),
        out_specs=P("dp", None, None),
        check_vma=False,
    )
```

profile of v0, /device:TPU:0, one launch (start us, length us, event | category | flops | bytes accessed | tf_op | source)
XLA Modules:
  0.0 217.8 jit_solution(13402639496376472465)
XLA Ops:
  6.5 0.0 all-gather.3.cloned.1.call-start
  6.5 1.1 copy.46
  7.6 67.0 %multiply_reduce_fusion = (f32[32,8,6]{2,1,0:T(8,128)S(1)}, f32[32,8,6,2048]{3,2,1,0:T(8,128)}) fusion(bf16[32,2048,8,128]{3,2,1,0:T(8,128)(2,1)} %param.4, bf16[32,8,6,128]{3,0,2,1:T(8,128)(2,1)S(1)} %bitcast.14), kind=kOutput, calls=%fused_computation.5 | convolution fusion | flops 811596288 | bytes 147200000 | tf_op jit(solution)/shard_map/bgsd,bugd->bgsu/dot_general | solution.py:8
  74.6 7.8 %fusion.4 = f32[32,8,6]{2,1,0:T(8,128)S(1)} fusion(f32[32,8,6,2048]{3,2,1,0:T(8,128)} %get-tuple-element.11, f32[32,8,6]{2,1,0:T(8,128)S(1)} %get-tuple-element.10), kind=kLoop, calls=%fused_computation.6 | loop fusion | flops 9435648 | bytes 12595200 | tf_op jit(solution)/shard_map/reduce_sum | solution.py:17
  82.4 61.9 %fusion = f32[32,8,6,128]{3,2,1,0:T(8,128)S(1)} fusion(bf16[32,2048,8,128]{3,2,1,0:T(8,128)(2,1)} %param.5, f32[32,8,6,2048]{3,2,1,0:T(8,128)} %get-tuple-element.11, f32[32,8,6]{2,1,0:T(8,128)S(1)} %get-tuple-element.10), kind=kOutput, calls=%fused_computation | convolution fusion | flops 814743552 | bytes 147593216 | tf_op jit(solution)/shard_map/bgsu,bugd->bgsd/dot_general | solution.py:8
  144.3 1.7 copy.52
  146.0 1.7 copy.53
  147.7 0.4 pad_maximum_fusion
  148.1 1.8 copy.54
  149.9 0.0 all-gather.3.cloned.1.call-update
  149.9 46.6 %all-gather.3.cloned.1.call-done = f32[128,8,6,130]{3,1,2,0:T(8,128)} async-done(((f32[32,8,6,130]{3,1,2,0:T(8,128)}), f32[128,8,6,130]{3,1,2,0:T(8,128)}) %all-gather.3.cloned.1.call-update) | async-done | bytes 3194896 | tf_op jit(solution)/shard_map/all_gather | solution.py:28
  196.5 5.9 %fusion.14 = (f32[4,32,8,6,1]{4,2,3,1,0:T(8,128)}, f32[32,8,6]{1,2,0:T(8,128)S(1)}, f32[4,32,8,6,1]{4,2,3,1,0:T(8,128)S(1)}) fusion(f32[4,32,8,6,130]{4,2,3,1,0:T(8,128)} %bitcast.12), kind=kLoop, calls=%fused_computation.21 | loop fusion | flops 4608 | bytes 104448 | tf_op jit(solution)/shard_map/slice | solution.py:21
  202.4 2.7 %copy.68 = f32[4,32,8,6,1]{1,2,4,3,0:T(8,128)S(1)} copy(f32[4,32,8,6,1]{4,2,3,1,0:T(8,128)} %get-tuple-element.5) | data formatting | bytes 49152
  205.1 0.1 copy.70
  205.2 1.5 copy.67
  206.8 0.2 copy.56
  207.0 2.5 %fusion.9 = f32[32,8,6,128]{3,1,2,0:T(8,128)S(1)} fusion(f32[4,32,8,6,130]{4,2,3,1,0:T(8,128)} %bitcast.13, f32[4,32,8,6]{2,3,1,0:T(8,128)S(1)} %copy.56), kind=kLoop, calls=%fused_computation.11 | loop fusion | flops 1376256 | bytes 3956736 | tf_op jit(solution)/shard_map/reduce_sum | solution.py:23
  209.5 0.3 copy.58
  209.8 0.3 fusion.10
  210.1 0.9 copy.61
  (3 shorter events, 0.0 us)
Async XLA Ops:
  6.5 190.0 %all-gather.3.cloned.1.call-start = ((), (), s32[]{:S(2)}) async-start(), calls=%async_computation | async-start | bytes 7864320 | tf_op jit(solution)/shard_map/all_gather | solution.py:28
Sparse Core Ops, SparseCore 0:
  150.0 46.4 all-gather.2
where the time goes:
time: 218 us
  matrix products  129 us (59%)
  waiting for transfers between devices  46.6 us (21%)
  other arithmetic  16.9 us (8%)
  between operations  13.5 us (6%)
  local copies, waits for them, and re-layouts  11.9 us (5%)
    dot_general x2, matrix products, einsum(): return jnp.einsum(form, a.astype(jnp.float32), b.astype(jnp.float32))  129 us
    all_gather x1, waiting for transfers between devices, step(): return together(lax.all_gather(part_of(q, k, v), 'sp')).reshape(q.shape)  46.6 us
    reduce_sum x1, other arithmetic, part_of(): jnp.sum(weights, -1, keepdims=True)  7.83 us
    slice x1, other arithmetic, together(): seen, total, high = (parts[..., :-2], parts[..., -2:-1], parts[..., -1:])  5.88 us
    unnamed x4, local copies, waits for them, and re-layouts  5.41 us
  transfers between devices with their start and end apart: 1, of which 1 were waited for; matrix products, arithmetic and copies ran while one was open for 0% of the time, Pallas kernels for 0%

commit v1 on v0

v1 whole, which is shorter than its diff:
```python
import functools

import jax
import jax.numpy as jnp
from jax import lax
from jax.experimental import pallas as pl
from jax.experimental.pallas import tpu as pltpu
from jax.sharding import PartitionSpec as P

SLOTS = 3
LAG = 3
ROWS = 512
HALF = ROWS // 2
LOG2E = 1.4426950408889634


def iota(shape, axis):
    return lax.broadcasted_iota(jnp.int32, shape, axis)


def order(shape, axis):
    r = iota(shape, axis)
    j = r >> 3
    return (((r & 7) + j) & 7) * 6 + j


def kernel(
    devices, scale, q_ref, k_hbm, v_hbm, out_ref, kbuf, vbuf, sbuf, hbuf, qp, seen, stats, ksem, vsem, osend, ssend, orecv, srecv
):
    batch, queries, head = q_ref.shape
    members = queries // 8
    rows = k_hbm.shape[1]
    steps = rows // ROWS
    me = lax.axis_index("sp")

    def fetch_k(b):
        return pltpu.make_async_copy(k_hbm.at[b], kbuf.at[lax.rem(b, SLOTS)], ksem.at[lax.rem(b, SLOTS)])

    def fetch_v(b):
        return pltpu.make_async_copy(v_hbm.at[b], vbuf.at[lax.rem(b, SLOTS)], vsem.at[lax.rem(b, SLOTS)])

    for b in range(SLOTS):
        fetch_k(b).start()
        fetch_v(b).start()

    barrier = pltpu.get_barrier_semaphore()
    for hop in range(1, devices):
        pl.semaphore_signal(barrier, inc=1, device_id={"sp": lax.rem(me + hop, devices)})
    pl.semaphore_wait(barrier, devices - 1)

    def sends(b):
        copies = []
        for hop in range(1, devices):
            peer = {"sp": lax.rem(me + hop, devices)}
            copies.append(
                pltpu.make_async_remote_copy(
                    seen.at[me, b], seen.at[me, b], osend.at[hop - 1, lax.rem(b, 2)], orecv.at[hop - 1, b], device_id=peer
                )
            )
            copies.append(
                pltpu.make_async_remote_copy(
                    stats.at[me, b], stats.at[me, b], ssend.at[hop - 1, lax.rem(b, 2)], srecv.at[hop - 1, b], device_id=peer
                )
            )
        return copies

    def masks(lanes):
        return [((iota((8, lanes), 0) + j) & 7) == (iota((8, lanes), 1) & 7) for j in range(members)]

    def roll_all(x, op):
        for shift in (8, 16, 32, 64):
            x = op(x, pltpu.roll(x, shift, 1))
        return x

    pick = jnp.where(order((queries, queries), 0) == iota((queries, queries), 1), 1.0, 0.0).astype(jnp.bfloat16)

    def permute(b, _):
        qp[b] = jnp.dot(pick, q_ref[b], preferred_element_type=jnp.float32).astype(jnp.bfloat16)
        return 0

    lax.fori_loop(0, batch, permute, 0)

    def query_block(b):
        q = qp[b]
        zero = jnp.zeros_like(q)
        return jnp.concatenate([jnp.concatenate([q, zero], 1), jnp.concatenate([zero, q], 1)], 0)

    def scores_step(qb, sel, slot, t, b2, high):
        r = t * ROWS
        k2 = jnp.concatenate([kbuf[slot, pl.ds(r, HALF), :], kbuf[slot, pl.ds(r + HALF, HALF), :]], 1)
        s = lax.dot_general(qb, k2, (((1,), (1,)), ((), ())), preferred_element_type=jnp.float32)
        for half in range(2):
            base = half * queries
            x = s[base : base + 8]
            for j in range(1, members):
                x = jnp.where(sel[j], s[base + 8 * j : base + 8 * j + 8], x)
            sbuf[b2, :, pl.ds(r + half * HALF, HALF)] = x
            for c in range(0, HALF, 128):
                high = jnp.maximum(high, x[:, c : c + 128])
        return high

    def weights_step(spread, slot, t, b2, top, total):
        r = t * ROWS
        blocks = []
        for half in range(2):
            x = sbuf[b2, :, pl.ds(r + half * HALF, HALF)]
            w = jnp.exp2(x * scale - jnp.concatenate([top] * (HALF // 128), 1))
            for c in range(0, HALF, 128):
                total = total + w[:, c : c + 128]
            w16 = jnp.concatenate([w, w], 0).astype(jnp.bfloat16)
            blocks += [w16 * m for m in spread]
        v2 = jnp.concatenate([vbuf[slot, pl.ds(r, HALF), :], vbuf[slot, pl.ds(r + HALF, HALF), :]], 1)
        return jnp.dot(jnp.concatenate(blocks, 0), v2, preferred_element_type=jnp.float32), total

    def start_high():
        return jnp.full((8, 128), -jnp.inf, jnp.float32)

    def spreads():
        m = [jnp.where(x, 1.0, 0.0) for x in masks(HALF)]
        return [jnp.concatenate([m[2 * j], m[2 * j + 1]], 0).astype(jnp.bfloat16) for j in range(members // 2)]

    def finish(b, acc, total, top):
        o = acc[:queries, :head] + acc[queries:, head:]
        seen[me, b] = o.astype(jnp.bfloat16)
        stats[me, b] = jnp.where(iota((8, 128), 1) < 64, top, roll_all(total, jnp.add))

    def body(b, last):
        slot_v = lax.rem(b, SLOTS)
        now, later = lax.rem(b, 2), lax.rem(b + 1, 2)
        top = roll_all(hbuf[now], jnp.maximum) * scale
        spread = spreads()
        acc = None
        total = jnp.zeros((8, 128), jnp.float32)
        if not last:
            slot_k = lax.rem(b + 1, SLOTS)
            sel = masks(HALF)
            qb = query_block(b + 1)
            high = start_high()
        for t in range(steps):
            if not last:
                high = scores_step(qb, sel, slot_k, t, later, high)
            part, total = weights_step(spread, slot_v, t, now, top, total)
            acc = part if acc is None else acc + part
        if not last:
            hbuf[later] = high
        finish(b, acc, total, top)

    unpick = jnp.where(order((queries, queries), 1) == iota((queries, queries), 0), 1.0, 0.0).astype(jnp.bfloat16)

    def combine(b):
        for hop in range(1, devices):
            src = lax.rem(me + devices - hop, devices)
            pltpu.make_async_copy(seen.at[src, b], seen.at[src, b], orecv.at[hop - 1, b]).wait()
            pltpu.make_async_copy(stats.at[src, b], stats.at[src, b], srecv.at[hop - 1, b]).wait()
        tiles = [stats[d, b] for d in range(devices)]
        top = functools.reduce(jnp.maximum, tiles)
        ratio = [jnp.exp2(x - top) for x in tiles]
        whole = functools.reduce(jnp.add, [pltpu.roll(x, 64, 1) * e for x, e in zip(tiles, ratio)])
        ratio = [e / whole for e in ratio]
        out = []
        o = [seen[d, b].astype(jnp.float32) for d in range(devices)]
        for j in range(members):
            lane = (iota((8, 128), 0) + j) & 7
            rows_j = [
                x[8 * j : 8 * j + 8] * jnp.take_along_axis(e, lane, axis=1, mode="promise_in_bounds") for x, e in zip(o, ratio)
            ]
            out.append(functools.reduce(jnp.add, rows_j))
        mixed = jnp.concatenate(out, 0).astype(jnp.bfloat16)
        out_ref[b] = jnp.dot(unpick, mixed, preferred_element_type=jnp.float32).astype(jnp.bfloat16)

    fetch_k(0).wait()
    sel = masks(HALF)
    qb = query_block(0)
    high = start_high()
    for t in range(steps):
        high = scores_step(qb, sel, 0, t, 0, high)
    hbuf[0] = high

    def loop(b, _):
        fetch_k(b + 1).wait()
        fetch_v(b).wait()

        @pl.when(b + SLOTS < batch)
        def _():
            fetch_k(b + SLOTS).start()

        @pl.when((b >= 1) & (b - 1 + SLOTS < batch))
        def _():
            fetch_v(b - 1 + SLOTS).start()

        @pl.when(b >= 1)
        def _():
            @pl.when(b >= 3)
            def _():
                for c in sends(b - 3):
                    c.wait_send()

            for c in sends(b - 1):
                c.start()

        body(b, False)

        @pl.when(b >= LAG)
        def _():
            combine(b - LAG)

        return 0

    lax.fori_loop(0, batch - 1, loop, 0)

    last = batch - 1
    for c in sends(last - 3):
        c.wait_send()
    for c in sends(last - 1):
        c.start()
    fetch_v(last).wait()
    body(last, True)
    for c in sends(last - 2):
        c.wait_send()
    for c in sends(last):
        c.start()
    for b in range(batch - 1 - LAG, batch):
        combine(b)
    for b in (last - 1, last):
        for c in sends(b):
            c.wait_send()


def attend(mesh, q, k, v):
    batch, tokens, heads, head = k.shape
    devices = mesh.shape["sp"]
    queries = q.shape[1]
    rows = tokens * heads
    bf16, f32 = jnp.bfloat16, jnp.float32
    any_space = pl.BlockSpec(memory_space=pl.ANY)
    vmem = pl.BlockSpec(memory_space=pltpu.VMEM)
    return pl.pallas_call(
        functools.partial(kernel, devices, head**-0.5 * LOG2E),
        out_shape=jax.ShapeDtypeStruct(q.shape, bf16),
        in_specs=[vmem, any_space, any_space],
        out_specs=vmem,
        scratch_shapes=[
            pltpu.VMEM((SLOTS, rows, head), bf16),
            pltpu.VMEM((SLOTS, rows, head), bf16),
            pltpu.VMEM((2, 8, rows), f32),
            pltpu.VMEM((2, 8, 128), f32),
            pltpu.VMEM((batch, queries, head), bf16),
            pltpu.VMEM((devices, batch, queries, head), bf16),
            pltpu.VMEM((devices, batch, 8, 128), f32),
            pltpu.SemaphoreType.DMA((SLOTS,)),
            pltpu.SemaphoreType.DMA((SLOTS,)),
            pltpu.SemaphoreType.DMA((devices - 1, 2)),
            pltpu.SemaphoreType.DMA((devices - 1, 2)),
            pltpu.SemaphoreType.DMA((devices - 1, batch)),
            pltpu.SemaphoreType.DMA((devices - 1, batch)),
        ],
        compiler_params=pltpu.CompilerParams(collective_id=0, has_side_effects=True, vmem_limit_bytes=60 * 2**20),
        cost_estimate=pl.CostEstimate(flops=8 * 4 * q.size * tokens, bytes_accessed=2 * 2 * k.size, transcendentals=q.shape[0] * queries * tokens),
    )(q, k.reshape(batch, rows, head), v.reshape(batch, rows, head))


def solution(mesh):
    return jax.shard_map(
        functools.partial(attend, mesh),
        mesh=mesh,
        in_specs=(P("dp", None, None), P("dp", "sp", None, None), P("dp", "sp", None, None)),
        out_specs=P("dp", None, None),
        check_vma=False,
    )
```

time: 218 us -> 118 us (0.54)
  matrix products: 129 us -> 0 us
  Pallas kernels: 0 us -> 116 us
  waiting for transfers between devices: 46.6 us -> 0 us
  other arithmetic: 16.9 us -> 0 us
  between operations: 13.5 us -> 0.01 us
  local copies, waits for them, and re-layouts: 11.9 us -> 1.77 us
    dot_general x2 -> x0, matrix products: 129 us -> none  [einsum(): return jnp.einsum(form, a.astype(jnp.float32), b.astype(jnp.float32))]
    pallas_call x0 -> x1, Pallas kernels: none -> 116 us  [attend(): pl.pallas_call(functools.partial(kernel, devices, head ** (-0.5) * LOG2E)...]
    all_gather x1 -> x0, waiting for transfers between devices: 46.6 us -> none  [step(): return together(lax.all_gather(part_of(q, k, v), 'sp')).reshape(q.shape)]
    reduce_sum x3 -> x0, other arithmetic: 10.3 us -> none  [the longest x1 7.83 us: part_of(): jnp.sum(weights, -1, keepdims=True)]
    slice x1 -> x0, other arithmetic: 5.88 us -> none  [together(): seen, total, high = (parts[..., :-2], parts[..., -2:-1], parts[..., -1:])]
    unnamed x4 -> x1, local copies, waits for them, and re-layouts: 5.41 us -> 1.77 us
    broadcast_in_dim x2 -> x0, local copies, waits for them, and re-layouts: 3.33 us -> none  [the longest x1 1.66 us: part_of(): jnp.sum(weights, -1, keepdims=True)]
  transfers between devices with their start and end apart: 1 -> 0, of which waited for: 1 -> 0; matrix products, arithmetic and copies ran while one was open for 0% -> 0% of each run, Pallas kernels for 0% -> 0%
where the time goes in v1:
time: 118 us
  Pallas kernels  116 us (98%)
  local copies, waits for them, and re-layouts  1.77 us (2%)
    pallas_call x1, Pallas kernels, attend(): pl.pallas_call(functools.partial(kernel, devices, head ** (-0.5) * LOG2E)...  116 us

profile of v1, /device:TPU:0, one launch (start us, length us, event | category | flops | bytes accessed | tf_op | source)
XLA Modules:
  0.0 117.9 jit_solution(2395368296971515014)
XLA Ops:
  0.0 116.1 %shard_map.37 = bf16[32,48,128]{2,1,0:T(8,128)(2,1)} custom-call(bf16[32,48,128]{2,1,0:T(8,128)(2,1)} %q_ref.1, bf16[32,16384,128]{2,1,0:T(8,128)(2,1)} %bitcast.k_hbm, bf16[32,16384,128]{2,1,0:T(8,128)(2,1)} %bitcast.1.v_hbm), custom_call_target="tpu_custom_call" | custom-call | flops 12884901888 | bytes 268435456 | tf_op jit(solution)/shard_map/pallas_call | solution.py:237
  116.1 1.8 %copy.5 = bf16[32,48,128]{2,1,0:T(8,128)(2,1)} copy(bf16[32,48,128]{2,1,0:T(8,128)(2,1)} %shard_map.37) | data formatting | bytes 786432

commit v2 on v1

v2 whole, which is shorter than its diff:
```python
import functools

import jax
import jax.numpy as jnp
from jax import lax
from jax.experimental import pallas as pl
from jax.experimental.pallas import tpu as pltpu
from jax.sharding import PartitionSpec as P

SLOTS = 5
GROUP = 8
ROWS = 512
HALF = ROWS // 2
LOG2E = 1.4426950408889634


def iota(shape, axis):
    return lax.broadcasted_iota(jnp.int32, shape, axis)


def order(shape, axis):
    r = iota(shape, axis)
    j = r >> 3
    return (((r & 7) + j) & 7) * 6 + j


def kernel(
    devices, scale, q_ref, k_hbm, v_hbm, out_ref, kbuf, vbuf, sbuf, hbuf, acc_ref, sums, qp, seen, stats, parts, numbers, ksem, vsem,
    osend, ssend, orecv, srecv, rsend, rrecv, lsend, tsend, lrecv, trecv,
):
    batch, queries, head = q_ref.shape
    members = queries // 8
    rows = k_hbm.shape[1]
    steps = rows // ROWS
    groups = batch // devices - 1
    me = lax.axis_index("sp")

    def fetch_k(b):
        return pltpu.make_async_copy(k_hbm.at[b], kbuf.at[lax.rem(b, SLOTS)], ksem.at[lax.rem(b, SLOTS)])

    def fetch_v(b):
        return pltpu.make_async_copy(v_hbm.at[b], vbuf.at[lax.rem(b, SLOTS)], vsem.at[lax.rem(b, SLOTS)])

    for b in range(SLOTS):
        fetch_k(b).start()
        fetch_v(b).start()

    barrier = pltpu.get_barrier_semaphore()
    for hop in range(1, devices):
        pl.semaphore_signal(barrier, inc=1, device_id={"sp": lax.rem(me + hop, devices)})
    pl.semaphore_wait(barrier, devices - 1)

    def peer(hop):
        return {"sp": lax.rem(me + hop, devices)}

    def behind(hop):
        return lax.rem(me + devices - hop, devices)

    def remote(src, dst, send, recv, hop):
        return pltpu.make_async_remote_copy(src, dst, send, recv, device_id=peer(hop))

    def group_sends(g):
        copies = []
        for hop in range(1, devices):
            b = g * devices + lax.rem(me + hop, devices)
            n = hop - 1
            copies.append(remote(seen.at[b], parts.at[n, g], osend.at[n], orecv.at[n, g], hop))
            copies.append(remote(stats.at[b], numbers.at[n, g], ssend.at[n], srecv.at[n, g], hop))
        return copies

    def result_sends(g):
        at = out_ref.at[g * devices + me]
        return [remote(at, at, rsend.at[hop - 1], rrecv.at[hop - 1, g], hop) for hop in range(1, devices)]

    def last_sends(n):
        b = batch - devices + n
        copies = []
        for hop in range(1, devices):
            m = hop - 1
            copies.append(remote(seen.at[b], parts.at[m, groups + n], lsend.at[m, n], lrecv.at[m, n], hop))
            copies.append(remote(stats.at[b], numbers.at[m, groups + n], tsend.at[m, n], trecv.at[m, n], hop))
        return copies

    def masks(lanes):
        return [((iota((8, lanes), 0) + j) & 7) == (iota((8, lanes), 1) & 7) for j in range(members)]

    def roll_all(x, op):
        for shift in (8, 16, 32, 64):
            x = op(x, pltpu.roll(x, shift, 1))
        return x

    pick = jnp.where(order((queries, queries), 0) == iota((queries, queries), 1), 1.0, 0.0).astype(jnp.bfloat16)

    def permute(n, _):
        for b in range(8):
            b += n * 8
            qp[b] = jnp.dot(pick, q_ref[b], preferred_element_type=jnp.float32).astype(jnp.bfloat16)
        return 0

    lax.fori_loop(0, batch // 8, permute, 0)

    def query_block(b):
        q = qp[b]
        zero = jnp.zeros_like(q)
        return jnp.concatenate([jnp.concatenate([q, zero], 1), jnp.concatenate([zero, q], 1)], 0)

    def scores_step(qb, sel, slot, t, b2, high):
        r = t * ROWS
        k2 = jnp.concatenate([kbuf[slot, pl.ds(r, HALF), :], kbuf[slot, pl.ds(r + HALF, HALF), :]], 1)
        s = lax.dot_general(qb, k2, (((1,), (1,)), ((), ())), preferred_element_type=jnp.float32)
        for half in range(2):
            base = half * queries
            x = s[base : base + 8]
            for j in range(1, members):
                x = jnp.where(sel[j], s[base + 8 * j : base + 8 * j + 8], x)
            sbuf[b2, :, pl.ds(r + half * HALF, HALF)] = x
            for c in range(0, HALF, 128):
                high = jnp.maximum(high, x[:, c : c + 128])
        return high

    def weights_step(spread, slot, t, b2, top, total, acc):
        r = t * ROWS
        for half in range(2):
            at = pl.ds(r + half * HALF, HALF)
            w = jnp.exp2(sbuf[b2, :, at] * scale - jnp.concatenate([top] * (HALF // 128), 1))
            for c in range(0, HALF, 128):
                total = total + w[:, c : c + 128]
            w16 = jnp.concatenate([w, w], 0).astype(jnp.bfloat16)
            part = jnp.dot(
                jnp.concatenate([w16 * m for m in spread], 0), vbuf[slot, at, :], preferred_element_type=jnp.float32
            )
            acc = part if acc is None else acc + part
        return total, acc

    def start_high():
        return jnp.full((8, 128), -jnp.inf, jnp.float32)

    def spreads():
        m = [jnp.where(x, 1.0, 0.0) for x in masks(HALF)]
        return [jnp.concatenate([m[2 * j], m[2 * j + 1]], 0).astype(jnp.bfloat16) for j in range(members // 2)]

    def finish(b):
        seen[b] = acc_ref[...].astype(jnp.bfloat16)
        top, total = (pltpu.roll(x, 0, 1, stride=7, stride_axis=0) for x in (sums[0], roll_all(sums[1], jnp.add)))
        stats[b] = jnp.where(iota((8, 128), 1) < 64, top, total)

    def body(b, last):
        slot_v = lax.rem(b, SLOTS)
        now, later = lax.rem(b, 2), lax.rem(b + 1, 2)
        top = roll_all(hbuf[now], jnp.maximum) * scale
        spread = spreads()
        acc = None
        total = jnp.zeros((8, 128), jnp.float32)
        if not last:
            slot_k = lax.rem(b + 1, SLOTS)
            sel = masks(HALF)
            qb = query_block(b + 1)
            high = start_high()
        for g in range(0, steps, GROUP):
            if not last:
                for t in range(g, g + GROUP):
                    high = scores_step(qb, sel, slot_k, t, later, high)
            for t in range(g, g + GROUP):
                total, acc = weights_step(spread, slot_v, t, now, top, total, acc)
        if not last:
            hbuf[later] = high
        acc_ref[...] = acc
        sums[0] = top
        sums[1] = total

    unpick = jnp.where(order((queries, queries), 1) == iota((queries, queries), 0), 1.0, 0.0).astype(jnp.bfloat16)

    def combine(b, at):
        tiles, seens = [], []
        for d in range(devices):
            hop = lax.rem(me + devices - d, devices)
            far = jnp.maximum(hop - 1, 0)
            own = hop == 0
            tiles.append(jnp.where(own, stats[b], numbers[far, at]))
            seens.append(jnp.where(own, seen[b], parts[far, at]).astype(jnp.float32))
        top = functools.reduce(jnp.maximum, tiles)
        ratio = [jnp.exp2(x - top) for x in tiles]
        whole = functools.reduce(jnp.add, [pltpu.roll(x, 64, 1) * e for x, e in zip(tiles, ratio)])
        ratio = [e / whole for e in ratio]
        out = []
        for j in range(members):
            terms = [x[8 * j : 8 * j + 8] * jnp.broadcast_to(e[:, j : j + 1], (8, head)) for x, e in zip(seens, ratio)]
            out.append(functools.reduce(jnp.add, terms))
        mixed = jnp.concatenate(out, 0).astype(jnp.bfloat16)
        out_ref[b] = jnp.dot(unpick, mixed, preferred_element_type=jnp.float32).astype(jnp.bfloat16)

    def wait_recv(copies):
        for c in copies:
            c.wait_recv()

    def wait_send(copies):
        for c in copies:
            c.wait_send()

    def start(copies):
        for c in copies:
            c.start()

    def tick(t):
        @pl.when(t >= 1)
        def _():
            wait_send(group_sends(t - 1))

        @pl.when(t < groups)
        def _():
            start(group_sends(t))

        @pl.when(t >= 3)
        def _():
            wait_send(result_sends(t - 3))

        @pl.when(t >= 2)
        def _():
            start(result_sends(t - 2))

        @pl.when(t >= 1)
        def _():
            wait_recv(group_sends(t - 1))
            combine((t - 1) * devices + me, t - 1)

    acc_ref[...] = jnp.zeros_like(acc_ref)
    sums[...] = jnp.zeros_like(sums)

    fetch_k(0).wait()
    sel = masks(HALF)
    qb = query_block(0)
    high = start_high()
    for t in range(steps):
        high = scores_step(qb, sel, 0, t, 0, high)
    hbuf[0] = high

    def step(b):
        fetch_k(b + 1).wait()
        fetch_v(b).wait()

        @pl.when(b + SLOTS < batch)
        def _():
            fetch_k(b + SLOTS).start()

        @pl.when((b >= 1) & (b - 1 + SLOTS < batch))
        def _():
            fetch_v(b - 1 + SLOTS).start()

        finish(jnp.maximum(b - 1, 0))
        body(b, False)

    def loop(b, _):
        step(b)

        @pl.when((b >= devices) & (lax.rem(b, devices) == 0))
        def _():
            tick(lax.div(b, devices) - 1)

        return 0

    last = batch - 1
    lax.fori_loop(0, last - 2, loop, 0)
    step(last - 2)
    start(last_sends(0))
    step(last - 1)
    start(last_sends(1))
    tick(groups)
    finish(last - 1)
    fetch_v(last).wait()
    start(last_sends(2))
    body(last, True)
    finish(last)
    start(last_sends(3))
    wait_send(result_sends(groups - 2))
    start(result_sends(groups - 1))
    for n in range(devices):
        wait_recv(last_sends(n))
        combine(batch - devices + n, groups + n)
    for g in range(groups):
        wait_recv(result_sends(g))
    wait_send(result_sends(groups - 1))
    for n in range(devices):
        wait_send(last_sends(n))


def attend(mesh, q, k, v):
    batch, tokens, heads, head = k.shape
    devices = mesh.shape["sp"]
    queries = q.shape[1]
    rows = tokens * heads
    peers, groups, dma = devices - 1, batch // devices - 1, pltpu.SemaphoreType.DMA
    bf16, f32 = jnp.bfloat16, jnp.float32
    any_space = pl.BlockSpec(memory_space=pl.ANY)
    vmem = pl.BlockSpec(memory_space=pltpu.VMEM)
    return pl.pallas_call(
        functools.partial(kernel, devices, head**-0.5 * LOG2E),
        out_shape=jax.ShapeDtypeStruct(q.shape, bf16),
        in_specs=[vmem, any_space, any_space],
        out_specs=vmem,
        scratch_shapes=[
            pltpu.VMEM((SLOTS, rows, head), bf16),
            pltpu.VMEM((SLOTS, rows, head), bf16),
            pltpu.VMEM((2, 8, rows), f32),
            pltpu.VMEM((2, 8, 128), f32),
            pltpu.VMEM((queries, head), f32),
            pltpu.VMEM((2, 8, 128), f32),
            pltpu.VMEM((batch, queries, head), bf16),
            pltpu.VMEM((batch, queries, head), bf16),
            pltpu.VMEM((batch, 8, 128), f32),
            pltpu.VMEM((peers, groups + devices, queries, head), bf16),
            pltpu.VMEM((peers, groups + devices, 8, 128), f32),
            dma((SLOTS,)),
            dma((SLOTS,)),
            dma((peers,)),
            dma((peers,)),
            dma((peers, groups)),
            dma((peers, groups)),
            dma((peers,)),
            dma((peers, groups)),
            *[dma((peers, devices))] * 4,
        ],
        compiler_params=pltpu.CompilerParams(collective_id=0, has_side_effects=True, vmem_limit_bytes=60 * 2**20),
        cost_estimate=pl.CostEstimate(flops=8 * 4 * q.size * tokens, bytes_accessed=2 * 2 * k.size, transcendentals=q.shape[0] * queries * tokens),
    )(q, k.reshape(batch, rows, head), v.reshape(batch, rows, head))


def solution(mesh):
    return jax.shard_map(
        functools.partial(attend, mesh),
        mesh=mesh,
        in_specs=(P("dp", None, None), P("dp", "sp", None, None), P("dp", "sp", None, None)),
        out_specs=P("dp", None, None),
        check_vma=False,
    )
```

time: 118 us -> 91.6 us (0.78)
  Pallas kernels: 116 us -> 89.6 us
    pallas_call x1, Pallas kernels: 116 us -> 89.6 us  [attend(): pl.pallas_call(functools.partial(kernel, devices, head ** (-0.5) * LOG2E)...]
where the time goes in v2:
time: 91.6 us; the launch traced here: 91.4 us
  Pallas kernels  89.6 us (98%)
  local copies, waits for them, and re-layouts  1.77 us (2%)
    pallas_call x1, Pallas kernels, attend(): pl.pallas_call(functools.partial(kernel, devices, head ** (-0.5) * LOG2E)...  89.6 us

profile of v2, /device:TPU:0, one launch (start us, length us, event | category | flops | bytes accessed | tf_op | source)
XLA Modules:
  0.0 91.4 jit_solution(10221959101276140901)
XLA Ops:
  0.0 89.6 %shard_map.37 = bf16[32,48,128]{2,1,0:T(8,128)(2,1)} custom-call(bf16[32,48,128]{2,1,0:T(8,128)(2,1)} %q_ref.1, bf16[32,16384,128]{2,1,0:T(8,128)(2,1)} %bitcast.k_hbm, bf16[32,16384,128]{2,1,0:T(8,128)(2,1)} %bitcast.1.v_hbm), custom_call_target="tpu_custom_call" | custom-call | flops 12884901888 | bytes 268435456 | tf_op jit(solution)/shard_map/pallas_call | solution.py:295
  89.7 1.8 %copy.5 = bf16[32,48,128]{2,1,0:T(8,128)(2,1)} copy(bf16[32,48,128]{2,1,0:T(8,128)(2,1)} %shard_map.37) | data formatting | bytes 786432

commit v3 on v2

--- a/solution.py
+++ b/solution.py
@@ -25,14 +25,15 @@
 
 
 def kernel(
-    devices, scale, q_ref, k_hbm, v_hbm, out_ref, kbuf, vbuf, sbuf, hbuf, acc_ref, sums, qp, seen, stats, parts, numbers, ksem, vsem,
+    devices, scale, q_hbm, k_hbm, v_hbm, out_ref, q_ref, kbuf, vbuf, sbuf, hbuf, acc_ref, sums, qp, seen, stats, parts, numbers, qsem, ksem, vsem, psem,
     osend, ssend, orecv, srecv, rsend, rrecv, lsend, tsend, lrecv, trecv,
 ):
-    batch, queries, head = q_ref.shape
+    batch, queries, head = q_hbm.shape
     members = queries // 8
     rows = k_hbm.shape[1]
     steps = rows // ROWS
     groups = batch // devices - 1
+    last = batch - 1
     me = lax.axis_index("sp")
 
     def fetch_k(b):
@@ -41,9 +42,15 @@
     def fetch_v(b):
         return pltpu.make_async_copy(v_hbm.at[b], vbuf.at[lax.rem(b, SLOTS)], vsem.at[lax.rem(b, SLOTS)])
 
-    for b in range(SLOTS):
-        fetch_k(b).start()
-        fetch_v(b).start()
+    fetch_q = pltpu.make_async_copy(q_hbm, q_ref, qsem)
+    fetch_q.start()
+    def fetch_piece(n):
+        at = pl.ds(n * GROUP * ROWS, GROUP * ROWS)
+        return pltpu.make_async_copy(v_hbm.at[last, at], vbuf.at[last % SLOTS, at], psem.at[n])
+
+    fetch_k(0).start()
+    fetch_k(1).start()
+    fetch_v(0).start()
 
     barrier = pltpu.get_barrier_semaphore()
     for hop in range(1, devices):
@@ -70,7 +77,7 @@
 
     def result_sends(g):
         at = out_ref.at[g * devices + me]
-        return [remote(at, at, rsend.at[hop - 1], rrecv.at[hop - 1, g], hop) for hop in range(1, devices)]
+        return [remote(at, at, rsend.at[hop - 1, lax.rem(g, 2)], rrecv.at[hop - 1, g], hop) for hop in range(1, devices)]
 
     def last_sends(n):
         b = batch - devices + n
@@ -97,6 +104,7 @@
             qp[b] = jnp.dot(pick, q_ref[b], preferred_element_type=jnp.float32).astype(jnp.bfloat16)
         return 0
 
+    fetch_q.wait()
     lax.fori_loop(0, batch // 8, permute, 0)
 
     def query_block(b):
@@ -144,29 +152,33 @@
         top, total = (pltpu.roll(x, 0, 1, stride=7, stride_axis=0) for x in (sums[0], roll_all(sums[1], jnp.add)))
         stats[b] = jnp.where(iota((8, 128), 1) < 64, top, total)
 
-    def body(b, last):
-        slot_v = lax.rem(b, SLOTS)
-        now, later = lax.rem(b, 2), lax.rem(b + 1, 2)
-        top = roll_all(hbuf[now], jnp.maximum) * scale
-        spread = spreads()
-        acc = None
-        total = jnp.zeros((8, 128), jnp.float32)
-        if not last:
-            slot_k = lax.rem(b + 1, SLOTS)
+    def body(scores, weights, before=None):
+        if weights is not None:
+            slot_v, now = lax.rem(weights, SLOTS), lax.rem(weights, 2)
+            top = roll_all(hbuf[now], jnp.maximum) * scale
+            spread = spreads()
+            acc = None
+            total = jnp.zeros((8, 128), jnp.float32)
+        if scores is not None:
+            slot_k, later = lax.rem(scores, SLOTS), lax.rem(scores, 2)
             sel = masks(HALF)
-            qb = query_block(b + 1)
+            qb = query_block(scores)
             high = start_high()
-        for g in range(0, steps, GROUP):
-            if not last:
-                for t in range(g, g + GROUP):
+        for g in range(steps // GROUP):
+            if before is not None:
+                before(g)
+            if scores is not None:
+                for t in range(g * GROUP, g * GROUP + GROUP):
                     high = scores_step(qb, sel, slot_k, t, later, high)
-            for t in range(g, g + GROUP):
-                total, acc = weights_step(spread, slot_v, t, now, top, total, acc)
-        if not last:
+            if weights is not None:
+                for t in range(g * GROUP, g * GROUP + GROUP):
+                    total, acc = weights_step(spread, slot_v, t, now, top, total, acc)
+        if scores is not None:
             hbuf[later] = high
-        acc_ref[...] = acc
-        sums[0] = top
-        sums[1] = total
+        if weights is not None:
+            acc_ref[...] = acc
+            sums[0] = top
+            sums[1] = total
 
     unpick = jnp.where(order((queries, queries), 1) == iota((queries, queries), 0), 1.0, 0.0).astype(jnp.bfloat16)
 
@@ -210,9 +222,9 @@
         def _():
             start(group_sends(t))
 
-        @pl.when(t >= 3)
-        def _():
-            wait_send(result_sends(t - 3))
+        @pl.when(t >= 4)
+        def _():
+            wait_send(result_sends(t - 4))
 
         @pl.when(t >= 2)
         def _():
@@ -227,12 +239,10 @@
     sums[...] = jnp.zeros_like(sums)
 
     fetch_k(0).wait()
-    sel = masks(HALF)
-    qb = query_block(0)
-    high = start_high()
-    for t in range(steps):
-        high = scores_step(qb, sel, 0, t, 0, high)
-    hbuf[0] = high
+    for b in range(1, SLOTS - 1):
+        fetch_k(b + 1).start()
+        fetch_v(b).start()
+    body(0, None)
 
     def step(b):
         fetch_k(b + 1).wait()
@@ -242,12 +252,17 @@
         def _():
             fetch_k(b + SLOTS).start()
 
-        @pl.when((b >= 1) & (b - 1 + SLOTS < batch))
+        @pl.when(b - 1 + SLOTS < last)
         def _():
             fetch_v(b - 1 + SLOTS).start()
 
+        @pl.when(b - 1 + SLOTS == last)
+        def _():
+            for n in range(steps // GROUP):
+                fetch_piece(n).start()
+
         finish(jnp.maximum(b - 1, 0))
-        body(b, False)
+        body(b + 1, b)
 
     def loop(b, _):
         step(b)
@@ -258,27 +273,34 @@
 
         return 0
 
-    last = batch - 1
     lax.fori_loop(0, last - 2, loop, 0)
     step(last - 2)
     start(last_sends(0))
-    step(last - 1)
+    fetch_k(last).wait()
+    finish(last - 2)
+    body(last, None)
     start(last_sends(1))
-    tick(groups)
+    fetch_v(last - 1).wait()
+    body(None, last - 1)
     finish(last - 1)
-    fetch_v(last).wait()
     start(last_sends(2))
-    body(last, True)
+
+    def before(g):
+        fetch_piece(g).wait()
+
+    body(None, last, before)
     finish(last)
     start(last_sends(3))
-    wait_send(result_sends(groups - 2))
+    tick(groups)
+    wait_send(result_sends(groups - 3))
     start(result_sends(groups - 1))
     for n in range(devices):
         wait_recv(last_sends(n))
         combine(batch - devices + n, groups + n)
     for g in range(groups):
         wait_recv(result_sends(g))
-    wait_send(result_sends(groups - 1))
+    for g in range(groups - 2, groups):
+        wait_send(result_sends(g))
     for n in range(devices):
         wait_send(last_sends(n))
 
@@ -294,10 +316,11 @@
     vmem = pl.BlockSpec(memory_space=pltpu.VMEM)
     return pl.pallas_call(
         functools.partial(kernel, devices, head**-0.5 * LOG2E),
-        out_shape=jax.ShapeDtypeStruct(q.shape, bf16),
-        in_specs=[vmem, any_space, any_space],
+        out_shape=pltpu.VMEM(q.shape, bf16),
+        in_specs=[any_space] * 3,
         out_specs=vmem,
         scratch_shapes=[
+            pltpu.VMEM(q.shape, bf16),
             pltpu.VMEM((SLOTS, rows, head), bf16),
             pltpu.VMEM((SLOTS, rows, head), bf16),
             pltpu.VMEM((2, 8, rows), f32),
@@ -309,13 +332,15 @@
             pltpu.VMEM((batch, 8, 128), f32),
             pltpu.VMEM((peers, groups + devices, queries, head), bf16),
             pltpu.VMEM((peers, groups + devices, 8, 128), f32),
+            dma,
             dma((SLOTS,)),
             dma((SLOTS,)),
+            dma((rows // (GROUP * ROWS),)),
             dma((peers,)),
             dma((peers,)),
             dma((peers, groups)),
             dma((peers, groups)),
-            dma((peers,)),
+            dma((peers, 2)),
             dma((peers, groups)),
             *[dma((peers, devices))] * 4,
         ],

time: 91.6 us -> 89 us (0.972)
  Pallas kernels: 89.6 us -> 88.2 us
  local copies, waits for them, and re-layouts: 1.77 us -> 0.75 us
    pallas_call x1, Pallas kernels: 89.6 us -> 88.2 us  [attend(): pl.pallas_call(functools.partial(kernel, devices, head ** (-0.5) * LOG2E)...]
    unnamed x1, local copies, waits for them, and re-layouts: 1.77 us -> 0.75 us
where the time goes in v3:
time: 89 us; the launch traced here: 88.9 us
  Pallas kernels  88.2 us (99%)
    pallas_call x1, Pallas kernels, attend(): pl.pallas_call(functools.partial(kernel, devices, head ** (-0.5) * LOG2E)...  88.2 us

profile of v3, /device:TPU:0, one launch (start us, length us, event | category | flops | bytes accessed | tf_op | source)
XLA Modules:
  0.0 88.9 jit_solution(1933429729704127939)
XLA Ops:
  0.0 88.2 %shard_map.37 = bf16[32,48,128]{2,1,0:T(8,128)(2,1)S(1)} custom-call(bf16[32,48,128]{2,1,0:T(8,128)(2,1)} %q_hbm.1, bf16[32,16384,128]{2,1,0:T(8,128)(2,1)} %bitcast.k_hbm, bf16[32,16384,128]{2,1,0:T(8,128)(2,1)} %bitcast.1.v_hbm), custom_call_target="tpu_custom_call" | custom-call | flops 12884901888 | bytes 268435456 | tf_op jit(solution)/shard_map/pallas_call | solution.py:317
  88.2 0.7 copy.5

commit v4 on v3

--- a/solution.py
+++ b/solution.py
@@ -148,7 +148,13 @@
         return [jnp.concatenate([m[2 * j], m[2 * j + 1]], 0).astype(jnp.bfloat16) for j in range(members // 2)]
 
     def finish(b):
+        finish_seen(b)
+        finish_stats(b)
+
+    def finish_seen(b):
         seen[b] = acc_ref[...].astype(jnp.bfloat16)
+
+    def finish_stats(b):
         top, total = (pltpu.roll(x, 0, 1, stride=7, stride_axis=0) for x in (sums[0], roll_all(sums[1], jnp.add)))
         stats[b] = jnp.where(iota((8, 128), 1) < 64, top, total)
 
@@ -274,8 +280,12 @@
         return 0
 
     lax.fori_loop(0, last - 2, loop, 0)
-    step(last - 2)
+    fetch_k(last - 1).wait()
+    finish(last - 3)
+    body(last - 1, None)
     start(last_sends(0))
+    fetch_v(last - 2).wait()
+    body(None, last - 2)
     fetch_k(last).wait()
     finish(last - 2)
     body(last, None)
@@ -285,12 +295,17 @@
     finish(last - 1)
     start(last_sends(2))
 
+    pieces = steps // GROUP
+
     def before(g):
-        fetch_piece(g).wait()
+        for n in range(pieces - 1) if g == 0 else [g] if g == pieces - 1 else []:
+            fetch_piece(n).wait()
 
     body(None, last, before)
-    finish(last)
-    start(last_sends(3))
+    finish_seen(last)
+    start(last_sends(devices - 1)[0::2])
+    finish_stats(last)
+    start(last_sends(devices - 1)[1::2])
     tick(groups)
     wait_send(result_sends(groups - 3))
     start(result_sends(groups - 1))

time: 89 us -> 88.9 us (level)
  no operation moved by 1% of the time
where the time goes in v4:
time: 88.9 us; the launch traced here: 88.8 us
  Pallas kernels  88.1 us (99%)
    pallas_call x1, Pallas kernels, attend(): pl.pallas_call(functools.partial(kernel, devices, head ** (-0.5) * LOG2E)...  88.1 us

profile of v4, /device:TPU:0, one launch (start us, length us, event | category | flops | bytes accessed | tf_op | source)
XLA Modules:
  0.0 88.8 jit_solution(10737402296714333735)
XLA Ops:
  0.0 88.1 %shard_map.37 = bf16[32,48,128]{2,1,0:T(8,128)(2,1)S(1)} custom-call(bf16[32,48,128]{2,1,0:T(8,128)(2,1)} %q_hbm.1, bf16[32,16384,128]{2,1,0:T(8,128)(2,1)} %bitcast.k_hbm, bf16[32,16384,128]{2,1,0:T(8,128)(2,1)} %bitcast.1.v_hbm), custom_call_target="tpu_custom_call" | custom-call | flops 12884901888 | bytes 268435456 | tf_op jit(solution)/shard_map/pallas_call | solution.py:332
  88.1 0.7 copy.5

commit v5 on v4

--- a/solution.py
+++ b/solution.py
@@ -118,8 +118,8 @@
         s = lax.dot_general(qb, k2, (((1,), (1,)), ((), ())), preferred_element_type=jnp.float32)
         for half in range(2):
             base = half * queries
-            x = s[base : base + 8]
-            for j in range(1, members):
+            x = jnp.zeros((8, HALF), jnp.float32)
+            for j in range(members):
                 x = jnp.where(sel[j], s[base + 8 * j : base + 8 * j + 8], x)
             sbuf[b2, :, pl.ds(r + half * HALF, HALF)] = x
             for c in range(0, HALF, 128):

time: 88.9 us -> 88.9 us (level)
  no operation moved by 1% of the time
where the time goes in v5:
time: 88.9 us; the launch traced here: 88.8 us
  Pallas kernels  88.1 us (99%)
    pallas_call x1, Pallas kernels, attend(): pl.pallas_call(functools.partial(kernel, devices, head ** (-0.5) * LOG2E)...  88.1 us

profile of v5, /device:TPU:0, one launch (start us, length us, event | category | flops | bytes accessed | tf_op | source)
XLA Modules:
  0.0 88.8 jit_solution(13955422858654674496)
XLA Ops:
  0.0 88.1 %shard_map.37 = bf16[32,48,128]{2,1,0:T(8,128)(2,1)S(1)} custom-call(bf16[32,48,128]{2,1,0:T(8,128)(2,1)} %q_hbm.1, bf16[32,16384,128]{2,1,0:T(8,128)(2,1)} %bitcast.k_hbm, bf16[32,16384,128]{2,1,0:T(8,128)(2,1)} %bitcast.1.v_hbm), custom_call_target="tpu_custom_call" | custom-call | flops 12884901888 | bytes 268435456 | tf_op jit(solution)/shard_map/pallas_call | solution.py:332
  88.1 0.7 copy.5
